TPU v7x, 32 devices: a whole 2x2x4 slice. The times are simulated.
32 devices in a mesh: gx: 4 (over z), gy: 2 (over y), gz: 4 (over x, core).
Axes of the slice: x: 2, y: 2, z: 4, core: 2. Of those that a mesh axis runs over, the one named last changes fastest.
Arguments:
- hidden_acts: bfloat16 [4, 2, 4, 256, 16384], P('gz', 'gy', 'gx'), may hold values from -6 to 6
- output_grad: bfloat16 [4, 2, 4, 256, 32], P('gz', 'gy', 'gx'), may hold values from -6 to 6
- weights: bfloat16 [4, 2, 4, 32, 16384], P('gz', 'gy', 'gx'), may hold values from -6 to 6
- momentum: bfloat16 [4, 2, 4, 32, 16384], P('gz', 'gy', 'gx'), may hold values from -48 to 48
- worker_of_slot: int32 [32], replicated, may hold values from 0 to 31, each once
- round_shift: int32 [8], replicated, may hold values from 0 to 4, as said below
Outputs:
- mixed: bfloat16 [4, 2, 4, 32, 16384], P('gx', 'gy', 'gz')
- new_momentum: bfloat16 [4, 2, 4, 32, 16384], P('gz', 'gy', 'gx')
Inputs may be any that keep to these rules, and one draw needn't show every extreme that they name: `round_shift`: each entry is below log2 of 32, so offsets are powers of two below 32; some round has offset 32 / 2 and some round offset 1.
All inputs are finite; a program needn't handle non-finite values.
Results may differ from a plain program's by a relative error of at most 0.0081.
Values may be sent and summed in bfloat16 or wider, within the bound.
A program may use at most 64 MiB of HBM per device.

v0:
```python
import functools

import jax
import jax.numpy as jnp
from jax import lax
from jax.experimental import pallas as pl
from jax.experimental.pallas import tpu as pltpu
from jax.sharding import PartitionSpec as P

learn_rate = 0.01
beta_keep = 0.9
TILE = 16
GROUP = 2
MESH = pl.DeviceIdType.MESH


def iota(shape, axis):
    return lax.broadcasted_iota(jnp.int32, shape, axis)


def ones_where(mask):
    return jnp.where(mask, 1.0, 0.0).astype(jnp.bfloat16)


def exact_dot(a, b):
    return jnp.dot(a, b, preferred_element_type=jnp.float32)


def kernel(
    sizes,
    hidden_hbm,
    grad_ref,
    weight_hbm,
    moment_hbm,
    held_ref,
    shift_ref,
    out_ref,
    new_moment_ref,
    hidden,
    weight,
    moment,
    stage,
    recv,
    mixed,
    spread,
    hidden_sem,
    moment_sem,
    weight_sem,
    send_sem,
    recv_sem,
    back_send_sem,
    back_recv_sem,
):
    size_x, size_y, size_z = sizes
    workers = size_x * size_y * size_z
    columns, _, width = hidden.shape
    parts = out_ref.shape[0] // TILE
    chunks = recv.shape[0]
    rounds = shift_ref.shape[0]
    my_x, my_y, my_z = lax.axis_index("gx"), lax.axis_index("gy"), lax.axis_index("gz")
    me = (my_x * size_y + my_y) * size_z + my_z
    slot = my_x + size_x * (my_y + size_y * my_z)
    half_x = size_x // 2

    def target(step):
        per = workers // 2
        far = 1 - lax.div(step, per)
        rest = lax.rem(step, per)
        side = lax.div(my_x, half_x)
        other = far + side - 2 * far * side
        to_y = lax.rem(my_y + lax.rem(rest, size_y), size_y)
        to_z = lax.rem(my_z + lax.rem(lax.div(rest, size_y), size_z), size_z)
        to_x = other * half_x + lax.rem(my_x + lax.div(rest, size_y * size_z), half_x)
        return (to_x * size_y + to_y) * size_z + to_z

    def coordinates(device):
        return {
            "gx": lax.div(device, size_y * size_z),
            "gy": lax.rem(lax.div(device, size_z), size_y),
            "gz": lax.rem(device, size_z),
        }

    def column(step):
        return target(step) if columns == workers else lax.rem(me + step, columns)

    def loads(step):
        place = column(step)
        span = pl.ds(pl.multiple_of(place * width, 128), width)
        return [
            pltpu.make_async_copy(source.at[:, span], kept.at[place], sem.at[step])
            for source, kept, sem in (
                (hidden_hbm, hidden, hidden_sem),
                (moment_hbm, moment, moment_sem),
                (weight_hbm, weight, weight_sem),
            )
        ]

    def load(step, carry):
        for copy in loads(step):
            copy.start()
        return carry

    barrier = pltpu.get_barrier_semaphore()

    def greet(step, carry):
        device = target(step)

        @pl.when(device != me)
        def _():
            pl.semaphore_signal(
                barrier, inc=1, device_id=coordinates(device), device_id_type=MESH
            )

        return carry

    lax.fori_loop(0, workers, greet, 0)
    lax.fori_loop(0, columns, load, 0)
    grad_rows = grad_ref[...]
    def place_of(part, where):
        block = part * columns
        return block // workers, block % workers + where

    def send(part, where):
        chunk, device = place_of(part, where)

        @pl.when(device != me)
        def _():
            pltpu.make_async_remote_copy(
                src_ref=stage.at[part, where],
                dst_ref=recv.at[chunk, slot],
                send_sem=send_sem.at[chunk],
                recv_sem=recv_sem.at[chunk],
                device_id=coordinates(device),
                device_id_type=MESH,
            ).start()

    early = [part for part in range(parts) if place_of(part, 0)[0] == 0]
    late = [part for part in range(parts) if place_of(part, 0)[0] > 0]

    def compute(group):
        steps = [group * GROUP + k for k in range(GROUP)]
        for step in steps:
            for copy in loads(step):
                copy.wait()
        places = [column(step) for step in steps]
        grads = [exact_dot(grad_rows, hidden[where]) for where in places]
        for where, grad in zip(places, grads):
            span = pl.ds(pl.multiple_of(where * width, 128), width)
            velocity = beta_keep * moment[where].astype(jnp.float32) + grad
            new_moment_ref[:, span] = velocity.astype(jnp.bfloat16)
            stepped = (weight[where].astype(jnp.float32) - learn_rate * velocity).astype(
                jnp.bfloat16
            )
            for part in range(parts):
                piece = stepped[part * TILE : (part + 1) * TILE]
                stage[part, where] = piece
                chunk, device = place_of(part, where)

                @pl.when(device == me)
                def _():
                    recv[chunk, slot] = piece

    def send_early(group):
        for k in range(GROUP):
            for part in early:
                send(part, column(group * GROUP + k))

    def compute_and_send(group, carry):
        compute(group)
        send_early(group - 1)
        return carry

    groups = columns // GROUP
    compute(jnp.int32(0))
    pl.semaphore_wait(barrier, workers - 1)
    send_early(jnp.int32(0))
    compute(jnp.int32(1))
    lax.fori_loop(2, groups, compute_and_send, 0)
    send_early(jnp.int32(groups - 1))
    for part in late:
        lax.fori_loop(0, columns, lambda step, c: (send(part, column(step)), c)[1], 0)

    square = (workers, workers)
    gap = lax.rem(iota(square, 0) - iota(square, 1) + workers, workers)
    level = jnp.full(square, -1, jnp.int32)
    for power in range(workers.bit_length() - 1):
        level = jnp.where(gap == 1 << power, power, level)
    table = ones_where(held_ref[...] == iota(square, 0))
    for step in range(rounds):
        turn = ones_where((gap == 0) | (level == shift_ref[step]))
        table = exact_dot(turn, table).astype(jnp.bfloat16)
    distinct = workers // 2
    table = (table[:distinct].astype(jnp.float32) * 0.5**rounds).astype(jnp.bfloat16)
    wide = (workers, workers * TILE)
    table = exact_dot(table, ones_where(iota(wide, 1) // TILE == iota(wide, 0))).astype(
        jnp.bfloat16
    )
    height = min(256, distinct * TILE)

    def fill(step, carry):
        tall = (height, distinct)
        pick = ones_where((iota(tall, 0) + step * height) // TILE == iota(tall, 1))
        full = (height, workers * TILE)
        same = iota(full, 0) % TILE == iota(full, 1) % TILE
        spread[pl.ds(pl.multiple_of(step * height, height), height), :] = jnp.where(
            same, exact_dot(pick, table), 0.0
        ).astype(jnp.bfloat16)
        return carry

    lax.fori_loop(0, distinct * TILE // height, fill, 0)

    def pieces_wait(sem):
        ref = recv.at[0, pl.ds(0, workers - 1)]
        pltpu.make_async_copy(ref, ref, sem).wait()

    for chunk in range(chunks):
        pieces_wait(recv_sem.at[chunk])
        got = recv[chunk].reshape(workers * TILE, width)

        def blend(step, carry):
            result = exact_dot(
                spread[pl.ds(pl.multiple_of(step * height, height), height), :], got
            )
            mixed[chunk, pl.ds(step * (height // TILE), height // TILE)] = result.astype(
                jnp.bfloat16
            ).reshape(height // TILE, TILE, width)
            return carry

        lax.fori_loop(0, distinct * TILE // height, blend, 0)
        block = chunk * workers + me
        row = pl.multiple_of(lax.div(block, columns) * TILE, TILE)
        first = pl.multiple_of(lax.rem(block, columns) * width, 128)
        mine = (pl.ds(row, TILE), pl.ds(first, width))
        out_ref[mine] = mixed[chunk, lax.rem(me, distinct)]

        turned = workers // 2 if chunk == chunks - 1 else 0

        def back(step, carry):
            device = target(lax.rem(step + turned, workers))

            @pl.when(device != me)
            def _():
                pltpu.make_async_remote_copy(
                    src_ref=mixed.at[chunk, lax.rem(device, distinct)],
                    dst_ref=out_ref.at[mine],
                    send_sem=back_send_sem.at[chunk],
                    recv_sem=back_recv_sem.at[chunk],
                    device_id=coordinates(device),
                    device_id_type=MESH,
                ).start()

            return carry

        lax.fori_loop(0, workers, back, 0)

    for chunk in range(chunks):
        pieces_wait(send_sem.at[chunk])
        pieces_wait(back_send_sem.at[chunk])
        pieces_wait(back_recv_sem.at[chunk])


def store(mixed_ref, moment_ref, mixed_hbm, moment_hbm, sem):
    copies = [
        pltpu.make_async_copy(mixed_ref, mixed_hbm, sem.at[0]),
        pltpu.make_async_copy(moment_ref, moment_hbm, sem.at[1]),
    ]
    for copy in copies:
        copy.start()
    for copy in copies:
        copy.wait()


def shards(sizes, hidden_acts, output_grad, weights, momentum, worker_of_slot, round_shift):
    hidden = hidden_acts.reshape(hidden_acts.shape[-2:])
    grad_out = output_grad.reshape(output_grad.shape[-2:]).T
    weight = weights.reshape(weights.shape[-2:])
    moment = momentum.reshape(momentum.shape[-2:])
    workers = sizes[0] * sizes[1] * sizes[2]
    tokens, features = hidden.shape
    rows = weight.shape[0]
    parts = rows // TILE
    width = max(128, features // workers)
    columns = features // width
    chunks = parts * columns // workers
    distinct = workers // 2
    anywhere = pl.BlockSpec(memory_space=pl.ANY)
    vmem = pl.BlockSpec(memory_space=pltpu.VMEM)
    smem = pl.BlockSpec(memory_space=pltpu.SMEM)
    half = jnp.bfloat16
    mixed, new_moment = pl.pallas_call(
        functools.partial(kernel, sizes),
        out_shape=[pltpu.VMEM((rows, features), half)] * 2,
        in_specs=[anywhere, vmem, anywhere, anywhere, vmem, smem],
        out_specs=[vmem, vmem],
        scratch_shapes=[
            pltpu.VMEM((columns, tokens, width), half),
            pltpu.VMEM((columns, rows, width), half),
            pltpu.VMEM((columns, rows, width), half),
            pltpu.VMEM((parts, columns, TILE, width), half),
            pltpu.VMEM((chunks, workers, TILE, width), half),
            pltpu.VMEM((chunks, distinct, TILE, width), half),
            pltpu.VMEM((distinct * TILE, workers * TILE), half),
            pltpu.SemaphoreType.DMA((columns,)),
            pltpu.SemaphoreType.DMA((columns,)),
            pltpu.SemaphoreType.DMA((columns,)),
            pltpu.SemaphoreType.DMA((chunks,)),
            pltpu.SemaphoreType.DMA((chunks,)),
            pltpu.SemaphoreType.DMA((chunks,)),
            pltpu.SemaphoreType.DMA((chunks,)),
        ],
        compiler_params=pltpu.CompilerParams(
            collective_id=0, has_side_effects=True, vmem_limit_bytes=60 * 1024 * 1024
        ),
        name="step_and_gossip",
    )(hidden, grad_out, weight, moment, worker_of_slot.reshape(1, workers), round_shift)
    mixed, new_moment = pl.pallas_call(
        store,
        out_shape=[jax.ShapeDtypeStruct((rows, features), half)] * 2,
        in_specs=[anywhere, anywhere],
        out_specs=[anywhere, anywhere],
        scratch_shapes=[pltpu.SemaphoreType.DMA((2,))],
        name="store",
    )(
        pltpu.with_memory_space_constraint(mixed, pltpu.VMEM),
        pltpu.with_memory_space_constraint(new_moment, pltpu.VMEM),
    )
    return (mixed.reshape(weights.shape), new_moment.reshape(momentum.shape))


def solution(mesh):
    sizes = (mesh.shape["gx"], mesh.shape["gy"], mesh.shape["gz"])
    placed = (
        P("gz", "gy", "gx", None, None),
        P("gz", "gy", "gx", None, None),
        P("gz", "gy", "gx", None, None),
        P("gz", "gy", "gx", None, None),
        P(),
        P(),
    )
    return jax.shard_map(
        functools.partial(shards, sizes),
        mesh=mesh,
        in_specs=placed,
        out_specs=(P("gx", "gy", "gz", None, None), P("gz", "gy", "gx", None, None)),
        check_vma=False,
    )
```

profile of v0, /device:TPU:9, one launch (start us, length us, event | category | flops | bytes accessed | tf_op | source)
XLA Modules:
  0.0 56.0 jit_solution(11188414653617121120)
XLA Ops:
  0.6 54.0 %step_and_gossip.1 = (bf16[32,16384]{1,0:T(8,128)(2,1)S(1)}, bf16[32,16384]{1,0:T(8,128)(2,1)S(1)}) custom-call(bf16[256,16384]{1,0:T(8,128)(2,1)} %bitcast.9, bf16[32,256]{1,0:T(8,128)(2,1)} %bitcast.12, bf16[32,16384]{1,0:T(8,128)(2,1)} %bitcast.10, bf16[32,16384]{1,0:T(8,128)(2,1)} %bitcast.11, s32[1,32]{1,0:T(1,128)} %bitcast.13, s32[8]{0:T(128)} %shift_ref.1), custom_call_target="tpu_custom_call" | custom-call | tf_op jit(solution)/shard_map/step_and_gossip/pallas_call | solution.py:290
  54.7 1.3 %store.1 = (bf16[32,16384]{1,0:T(8,128)(2,1)}, bf16[32,16384]{1,0:T(8,128)(2,1)}) custom-call(bf16[32,16384]{1,0:T(8,128)(2,1)S(1)} %get-tuple-element.6.mixed_ref, bf16[32,16384]{1,0:T(8,128)(2,1)S(1)} %get-tuple-element.7.moment_ref), custom_call_target="tpu_custom_call" | custom-call | tf_op jit(solution)/shard_map/store/pallas_call | solution.py:316
where the time goes:
time: 56.3 us; the launch traced here: 56 us
  Pallas kernels  55.4 us (98%)
  between operations  0.64 us (1%)
    pallas_call x1, Pallas kernels, shards(): pl.pallas_call(functools.partial(kernel, sizes), out_shape=[pltpu.VMEM((r...  54 us
    pallas_call x1, Pallas kernels, shards(): pl.pallas_call(store, out_shape=[jax.ShapeDtypeStruct((rows, features), h...  1.33 us

commit v1 on v0

--- a/solution.py
+++ b/solution.py
@@ -11,7 +11,7 @@
 beta_keep = 0.9
 TILE = 16
 GROUP = 2
-MESH = pl.DeviceIdType.MESH
+LOGICAL = pl.DeviceIdType.LOGICAL
 
 
 def iota(shape, axis):
@@ -29,23 +29,26 @@
 def kernel(
     sizes,
     hidden_hbm,
-    grad_ref,
+    grad_hbm,
     weight_hbm,
     moment_hbm,
-    held_ref,
-    shift_ref,
+    held_hbm,
+    shift_hbm,
     out_ref,
     new_moment_ref,
     hidden,
+    grad_ref,
     weight,
     moment,
+    held_ref,
+    shift_ref,
     stage,
     recv,
     mixed,
     spread,
-    hidden_sem,
-    moment_sem,
-    weight_sem,
+    load_sem,
+    grad_sem,
+    table_sem,
     send_sem,
     recv_sem,
     back_send_sem,
@@ -53,69 +56,72 @@
 ):
     size_x, size_y, size_z = sizes
     workers = size_x * size_y * size_z
-    columns, _, width = hidden.shape
+    width = stage.shape[-1]
+    groups, _, span = hidden.shape
+    columns = stage.shape[1]
     parts = out_ref.shape[0] // TILE
     chunks = recv.shape[0]
     rounds = shift_ref.shape[0]
     my_x, my_y, my_z = lax.axis_index("gx"), lax.axis_index("gy"), lax.axis_index("gz")
     me = (my_x * size_y + my_y) * size_z + my_z
     slot = my_x + size_x * (my_y + size_y * my_z)
-    half_x = size_x // 2
+
+    plane = size_y * size_z
+    half = workers // 2
+    side = lax.div(me, half)
 
     def target(step):
-        per = workers // 2
-        far = 1 - lax.div(step, per)
-        rest = lax.rem(step, per)
-        side = lax.div(my_x, half_x)
-        other = far + side - 2 * far * side
-        to_y = lax.rem(my_y + lax.rem(rest, size_y), size_y)
-        to_z = lax.rem(my_z + lax.rem(lax.div(rest, size_y), size_z), size_z)
-        to_x = other * half_x + lax.rem(my_x + lax.div(rest, size_y * size_z), half_x)
-        return (to_x * size_y + to_y) * size_z + to_z
-
-    def coordinates(device):
-        return {
-            "gx": lax.div(device, size_y * size_z),
-            "gy": lax.rem(lax.div(device, size_z), size_y),
-            "gz": lax.rem(device, size_z),
-        }
+        return me ^ (workers - 1 - step)
+
+    def ranked(step):
+        far = 1 - lax.div(step, half)
+        turn = (side ^ far) * (size_x - 1)
+        layer = lax.div(lax.rem(step, half), plane) ^ turn
+        return layer * plane + ((me & (plane - 1)) ^ (plane - 1 - lax.rem(step, plane)))
 
     def column(step):
-        return target(step) if columns == workers else lax.rem(me + step, columns)
-
-    def loads(step):
-        place = column(step)
-        span = pl.ds(pl.multiple_of(place * width, 128), width)
+        return ranked(step) if columns == workers else (me ^ (columns - 1 - step)) & (columns - 1)
+
+    def pair(group):
+        return lax.div(column(group * GROUP), GROUP)
+
+    def loads(group):
+        place = pair(group)
+        cut = pl.ds(pl.multiple_of(place * span, 128), span)
         return [
-            pltpu.make_async_copy(source.at[:, span], kept.at[place], sem.at[step])
-            for source, kept, sem in (
-                (hidden_hbm, hidden, hidden_sem),
-                (moment_hbm, moment, moment_sem),
-                (weight_hbm, weight, weight_sem),
+            pltpu.make_async_copy(source.at[:, cut], kept.at[place], load_sem.at[group])
+            for source, kept in (
+                (hidden_hbm, hidden),
+                (moment_hbm, moment),
+                (weight_hbm, weight),
             )
         ]
 
-    def load(step, carry):
-        for copy in loads(step):
+    def load(group, carry):
+        for copy in loads(group):
             copy.start()
         return carry
 
     barrier = pltpu.get_barrier_semaphore()
 
     def greet(step, carry):
-        device = target(step)
-
-        @pl.when(device != me)
-        def _():
-            pl.semaphore_signal(
-                barrier, inc=1, device_id=coordinates(device), device_id_type=MESH
-            )
-
+        pl.semaphore_signal(
+            barrier, inc=1, device_id=target(step), device_id_type=LOGICAL
+        )
         return carry
 
-    lax.fori_loop(0, workers, greet, 0)
-    lax.fori_loop(0, columns, load, 0)
-    grad_rows = grad_ref[...]
+    grad_copy = pltpu.make_async_copy(grad_hbm, grad_ref, grad_sem.at[0])
+    table_copies = [
+        pltpu.make_async_copy(held_hbm, held_ref, table_sem.at[0]),
+        pltpu.make_async_copy(shift_hbm, shift_ref, table_sem.at[1]),
+    ]
+    grad_copy.start()
+    load(0, 0)
+    lax.fori_loop(0, workers - 1, greet, 0)
+    lax.fori_loop(1, groups, load, 0)
+    for copy in table_copies:
+        copy.start()
+
     def place_of(part, where):
         block = part * columns
         return block // workers, block % workers + where
@@ -130,35 +136,29 @@
                 dst_ref=recv.at[chunk, slot],
                 send_sem=send_sem.at[chunk],
                 recv_sem=recv_sem.at[chunk],
-                device_id=coordinates(device),
-                device_id_type=MESH,
+                device_id=device,
+                device_id_type=LOGICAL,
             ).start()
 
     early = [part for part in range(parts) if place_of(part, 0)[0] == 0]
     late = [part for part in range(parts) if place_of(part, 0)[0] > 0]
 
     def compute(group):
-        steps = [group * GROUP + k for k in range(GROUP)]
-        for step in steps:
-            for copy in loads(step):
-                copy.wait()
-        places = [column(step) for step in steps]
-        grads = [exact_dot(grad_rows, hidden[where]) for where in places]
-        for where, grad in zip(places, grads):
-            span = pl.ds(pl.multiple_of(where * width, 128), width)
-            velocity = beta_keep * moment[where].astype(jnp.float32) + grad
-            new_moment_ref[:, span] = velocity.astype(jnp.bfloat16)
-            stepped = (weight[where].astype(jnp.float32) - learn_rate * velocity).astype(
-                jnp.bfloat16
-            )
+        place = pair(group)
+        for copy in loads(group):
+            copy.wait()
+        grad = exact_dot(grad_ref[...], hidden[place])
+        velocity = beta_keep * moment[place].astype(jnp.float32) + grad
+        cut = pl.ds(pl.multiple_of(place * span, 128), span)
+        new_moment_ref[:, cut] = velocity.astype(jnp.bfloat16)
+        stepped = (weight[place].astype(jnp.float32) - learn_rate * velocity).astype(
+            jnp.bfloat16
+        )
+        for k in range(GROUP):
             for part in range(parts):
-                piece = stepped[part * TILE : (part + 1) * TILE]
-                stage[part, where] = piece
-                chunk, device = place_of(part, where)
-
-                @pl.when(device == me)
-                def _():
-                    recv[chunk, slot] = piece
+                stage[part, place * GROUP + k] = stepped[
+                    part * TILE : (part + 1) * TILE, k * width : (k + 1) * width
+                ]
 
     def send_early(group):
         for k in range(GROUP):
@@ -170,7 +170,7 @@
         send_early(group - 1)
         return carry
 
-    groups = columns // GROUP
+    grad_copy.wait()
     compute(jnp.int32(0))
     pl.semaphore_wait(barrier, workers - 1)
     send_early(jnp.int32(0))
@@ -179,6 +179,11 @@
     send_early(jnp.int32(groups - 1))
     for part in late:
         lax.fori_loop(0, columns, lambda step, c: (send(part, column(step)), c)[1], 0)
+    for chunk in range(chunks):
+        block = chunk * workers + me
+        recv[chunk, slot] = stage[lax.div(block, columns), lax.rem(block, columns)]
+    for copy in table_copies:
+        copy.wait()
 
     square = (workers, workers)
     gap = lax.rem(iota(square, 0) - iota(square, 1) + workers, workers)
@@ -236,7 +241,7 @@
         turned = workers // 2 if chunk == chunks - 1 else 0
 
         def back(step, carry):
-            device = target(lax.rem(step + turned, workers))
+            device = ranked(lax.rem(step + turned, workers))
 
             @pl.when(device != me)
             def _():
@@ -245,8 +250,8 @@
                     dst_ref=out_ref.at[mine],
                     send_sem=back_send_sem.at[chunk],
                     recv_sem=back_recv_sem.at[chunk],
-                    device_id=coordinates(device),
-                    device_id_type=MESH,
+                    device_id=device,
+                    device_id_type=LOGICAL,
                 ).start()
 
             return carry
@@ -283,26 +288,29 @@
     columns = features // width
     chunks = parts * columns // workers
     distinct = workers // 2
+    groups = columns // GROUP
     anywhere = pl.BlockSpec(memory_space=pl.ANY)
     vmem = pl.BlockSpec(memory_space=pltpu.VMEM)
-    smem = pl.BlockSpec(memory_space=pltpu.SMEM)
     half = jnp.bfloat16
     mixed, new_moment = pl.pallas_call(
         functools.partial(kernel, sizes),
         out_shape=[pltpu.VMEM((rows, features), half)] * 2,
-        in_specs=[anywhere, vmem, anywhere, anywhere, vmem, smem],
+        in_specs=[anywhere] * 6,
         out_specs=[vmem, vmem],
         scratch_shapes=[
-            pltpu.VMEM((columns, tokens, width), half),
-            pltpu.VMEM((columns, rows, width), half),
-            pltpu.VMEM((columns, rows, width), half),
+            pltpu.VMEM((groups, tokens, GROUP * width), half),
+            pltpu.VMEM((rows, tokens), half),
+            pltpu.VMEM((groups, rows, GROUP * width), half),
+            pltpu.VMEM((groups, rows, GROUP * width), half),
+            pltpu.VMEM((1, workers), jnp.int32),
+            pltpu.SMEM(round_shift.shape, jnp.int32),
             pltpu.VMEM((parts, columns, TILE, width), half),
             pltpu.VMEM((chunks, workers, TILE, width), half),
             pltpu.VMEM((chunks, distinct, TILE, width), half),
             pltpu.VMEM((distinct * TILE, workers * TILE), half),
-            pltpu.SemaphoreType.DMA((columns,)),
-            pltpu.SemaphoreType.DMA((columns,)),
-            pltpu.SemaphoreType.DMA((columns,)),
+            pltpu.SemaphoreType.DMA((groups,)),
+            pltpu.SemaphoreType.DMA((1,)),
+            pltpu.SemaphoreType.DMA((2,)),
             pltpu.SemaphoreType.DMA((chunks,)),
             pltpu.SemaphoreType.DMA((chunks,)),
             pltpu.SemaphoreType.DMA((chunks,)),

time: 56.3 us -> 53.6 us (0.952)
  Pallas kernels: 55.4 us -> 52.6 us
    pallas_call x1, Pallas kernels: 54 us -> 51.2 us  [shards(): pl.pallas_call(functools.partial(kernel, sizes), out_shape=[pltpu.VMEM((r...]
where the time goes in v1:
time: 53.6 us; the launch traced here: 53.2 us
  Pallas kernels  52.6 us (98%)
  between operations  0.64 us (1%)
    pallas_call x1, Pallas kernels, shards(): pl.pallas_call(functools.partial(kernel, sizes), out_shape=[pltpu.VMEM((r...  51.2 us
    pallas_call x1, Pallas kernels, shards(): pl.pallas_call(store, out_shape=[jax.ShapeDtypeStruct((rows, features), h...  1.33 us

profile of v1, /device:TPU:9, one launch (start us, length us, event | category | flops | bytes accessed | tf_op | source)
XLA Modules:
  0.0 53.2 jit_solution(5453128077803369876)
XLA Ops:
  0.6 51.2 %step_and_gossip.1 = (bf16[32,16384]{1,0:T(8,128)(2,1)S(1)}, bf16[32,16384]{1,0:T(8,128)(2,1)S(1)}) custom-call(bf16[256,16384]{1,0:T(8,128)(2,1)} %bitcast.9, bf16[32,256]{1,0:T(8,128)(2,1)} %bitcast.12, bf16[32,16384]{1,0:T(8,128)(2,1)} %bitcast.10, bf16[32,16384]{1,0:T(8,128)(2,1)} %bitcast.11, s32[1,32]{1,0:T(1,128)} %bitcast.13, s32[8]{0:T(128)} %shift_hbm.1), custom_call_target="tpu_custom_call" | custom-call | tf_op jit(solution)/shard_map/step_and_gossip/pallas_call | solution.py:295
  51.9 1.3 %store.1 = (bf16[32,16384]{1,0:T(8,128)(2,1)}, bf16[32,16384]{1,0:T(8,128)(2,1)}) custom-call(bf16[32,16384]{1,0:T(8,128)(2,1)S(1)} %get-tuple-element.6.mixed_ref, bf16[32,16384]{1,0:T(8,128)(2,1)S(1)} %get-tuple-element.7.moment_ref), custom_call_target="tpu_custom_call" | custom-call | tf_op jit(solution)/shard_map/store/pallas_call | solution.py:324

commit v2 on v1

--- a/solution.py
+++ b/solution.py
@@ -49,6 +49,8 @@
     load_sem,
     grad_sem,
     table_sem,
+    hub_sem,
+    all_sem,
     send_sem,
     recv_sem,
     back_send_sem,
@@ -69,9 +71,9 @@
     plane = size_y * size_z
     half = workers // 2
     side = lax.div(me, half)
-
-    def target(step):
-        return me ^ (workers - 1 - step)
+    lines = plane // GROUP
+    layers = (half if columns == workers else columns) // plane
+    my_line = lax.div(lax.rem(me, plane), GROUP)
 
     def ranked(step):
         far = 1 - lax.div(step, half)
@@ -79,11 +81,14 @@
         layer = lax.div(lax.rem(step, half), plane) ^ turn
         return layer * plane + ((me & (plane - 1)) ^ (plane - 1 - lax.rem(step, plane)))
 
-    def column(step):
-        return ranked(step) if columns == workers else (me ^ (columns - 1 - step)) & (columns - 1)
-
     def pair(group):
-        return lax.div(column(group * GROUP), GROUP)
+        side_groups = layers * lines
+        order = lax.rem(group, side_groups)
+        turn = my_line ^ ((lines - lax.div(order, layers)) & (lines - 1))
+        layer = lax.rem(order, layers)
+        if columns == workers:
+            layer = layer ^ ((side ^ (1 - lax.div(group, side_groups))) * (size_x - 1))
+        return layer * lines + turn
 
     def loads(group):
         place = pair(group)
@@ -103,11 +108,28 @@
         return carry
 
     barrier = pltpu.get_barrier_semaphore()
+    hub = my_x == 0
+
+    def signal(sem, device):
+        pl.semaphore_signal(sem, inc=1, device_id=device, device_id_type=LOGICAL)
+
+    mates = size_x * GROUP - 1
 
     def greet(step, carry):
-        pl.semaphore_signal(
-            barrier, inc=1, device_id=target(step), device_id_type=LOGICAL
-        )
+        mate = mates - step
+        signal(barrier, me ^ (lax.div(mate, GROUP) * plane + lax.rem(mate, GROUP)))
+        return carry
+
+    def greet_hub(step, carry):
+        signal(barrier, me ^ ((step + 1) * GROUP))
+        return carry
+
+    def tell_hub(step, carry):
+        signal(hub_sem, me ^ ((step + 1) * GROUP))
+        return carry
+
+    def tell_line(step, carry):
+        signal(all_sem, me + (step + 1) * plane)
         return carry
 
     grad_copy = pltpu.make_async_copy(grad_hbm, grad_ref, grad_sem.at[0])
@@ -117,7 +139,11 @@
     ]
     grad_copy.start()
     load(0, 0)
-    lax.fori_loop(0, workers - 1, greet, 0)
+    lax.fori_loop(0, mates, greet, 0)
+
+    @pl.when(hub)
+    def _():
+        lax.fori_loop(0, lines - 1, greet_hub, 0)
     lax.fori_loop(1, groups, load, 0)
     for copy in table_copies:
         copy.start()
@@ -160,25 +186,59 @@
                     part * TILE : (part + 1) * TILE, k * width : (k + 1) * width
                 ]
 
-    def send_early(group):
+    def send_parts(which, group):
         for k in range(GROUP):
-            for part in early:
-                send(part, column(group * GROUP + k))
+            for part in which:
+                send(part, pair(group) * GROUP + k)
+
+    def compute_ahead(group, carry):
+        compute(group)
+        return carry
+
+    def send_ahead(group, carry):
+        send_parts(early, group)
+        return carry
 
     def compute_and_send(group, carry):
         compute(group)
-        send_early(group - 1)
+        send_parts(early, group - 1)
+        return carry
+
+    def send_late(group, carry):
+        send_parts(late, group)
         return carry
 
     grad_copy.wait()
     compute(jnp.int32(0))
-    pl.semaphore_wait(barrier, workers - 1)
-    send_early(jnp.int32(0))
-    compute(jnp.int32(1))
-    lax.fori_loop(2, groups, compute_and_send, 0)
-    send_early(jnp.int32(groups - 1))
-    for part in late:
-        lax.fori_loop(0, columns, lambda step, c: (send(part, column(step)), c)[1], 0)
+    pl.semaphore_wait(barrier, mates + jnp.where(hub, lines - 1, 0))
+
+    @pl.when(hub)
+    def _():
+        lax.fori_loop(0, lines - 1, tell_hub, 0)
+
+    send_parts(early, jnp.int32(0))
+    for group in range(1, layers):
+        compute(jnp.int32(group))
+        send_parts(early, jnp.int32(group))
+    for group in range(layers):
+        send_parts(late, jnp.int32(group))
+    ahead = min(layers + 4, groups - 1)
+    lax.fori_loop(layers, ahead, compute_ahead, 0)
+
+    @pl.when(hub)
+    def _():
+        pl.semaphore_wait(hub_sem, lines - 1)
+        lax.fori_loop(0, size_x - 1, tell_line, 0)
+
+    @pl.when(jnp.logical_not(hub))
+    def _():
+        pl.semaphore_wait(all_sem, 1)
+
+    lax.fori_loop(layers, ahead - 1, send_ahead, 0)
+    lax.fori_loop(ahead, groups, compute_and_send, 0)
+    send_parts(early, jnp.int32(groups - 1))
+    if late:
+        lax.fori_loop(layers, groups, send_late, 0)
     for chunk in range(chunks):
         block = chunk * workers + me
         recv[chunk, slot] = stage[lax.div(block, columns), lax.rem(block, columns)]
@@ -311,6 +371,8 @@
             pltpu.SemaphoreType.DMA((groups,)),
             pltpu.SemaphoreType.DMA((1,)),
             pltpu.SemaphoreType.DMA((2,)),
+            pltpu.SemaphoreType.REGULAR,
+            pltpu.SemaphoreType.REGULAR,
             pltpu.SemaphoreType.DMA((chunks,)),
             pltpu.SemaphoreType.DMA((chunks,)),
             pltpu.SemaphoreType.DMA((chunks,)),

time: 53.6 us -> 52.2 us (0.974)
  Pallas kernels: 52.6 us -> 51.2 us
    pallas_call x1, Pallas kernels: 51.2 us -> 49.9 us  [shards(): pl.pallas_call(functools.partial(kernel, sizes), out_shape=[pltpu.VMEM((r...]
where the time goes in v2:
time: 52.2 us; the launch traced here: 51.9 us
  Pallas kernels  51.2 us (98%)
  between operations  0.64 us (1%)
    pallas_call x1, Pallas kernels, shards(): pl.pallas_call(functools.partial(kernel, sizes), out_shape=[pltpu.VMEM((r...  49.9 us
    pallas_call x1, Pallas kernels, shards(): pl.pallas_call(store, out_shape=[jax.ShapeDtypeStruct((rows, features), h...  1.33 us

profile of v2, /device:TPU:9, one launch (start us, length us, event | category | flops | bytes accessed | tf_op | source)
XLA Modules:
  0.0 51.9 jit_solution(1459420314150298548)
XLA Ops:
  0.6 49.9 %step_and_gossip.1 = (bf16[32,16384]{1,0:T(8,128)(2,1)S(1)}, bf16[32,16384]{1,0:T(8,128)(2,1)S(1)}) custom-call(bf16[256,16384]{1,0:T(8,128)(2,1)} %bitcast.9, bf16[32,256]{1,0:T(8,128)(2,1)} %bitcast.12, bf16[32,16384]{1,0:T(8,128)(2,1)} %bitcast.10, bf16[32,16384]{1,0:T(8,128)(2,1)} %bitcast.11, s32[1,32]{1,0:T(1,128)} %bitcast.13, s32[8]{0:T(128)} %shift_hbm.1), custom_call_target="tpu_custom_call" | custom-call | tf_op jit(solution)/shard_map/step_and_gossip/pallas_call | solution.py:355
  50.5 1.3 %store.1 = (bf16[32,16384]{1,0:T(8,128)(2,1)}, bf16[32,16384]{1,0:T(8,128)(2,1)}) custom-call(bf16[32,16384]{1,0:T(8,128)(2,1)S(1)} %get-tuple-element.6.mixed_ref, bf16[32,16384]{1,0:T(8,128)(2,1)S(1)} %get-tuple-element.7.moment_ref), custom_call_target="tpu_custom_call" | custom-call | tf_op jit(solution)/shard_map/store/pallas_call | solution.py:386

commit v3 on v2

--- a/solution.py
+++ b/solution.py
@@ -55,6 +55,10 @@
     recv_sem,
     back_send_sem,
     back_recv_sem,
+    far_recv_sem,
+    spare,
+    forward_send_sem,
+    forward_recv_sem,
 ):
     size_x, size_y, size_z = sizes
     workers = size_x * size_y * size_z
@@ -274,9 +278,41 @@
 
     lax.fori_loop(0, distinct * TILE // height, fill, 0)
 
-    def pieces_wait(sem):
-        ref = recv.at[0, pl.ds(0, workers - 1)]
+    def pieces_wait(sem, count=workers - 1):
+        ref = recv.at[0, pl.ds(0, count)]
         pltpu.make_async_copy(ref, ref, sem).wait()
+
+    def mirror(device):
+        return device ^ ((size_x - 1) * plane)
+
+    def home(chunk, owner):
+        block = chunk * workers + owner
+        row = pl.multiple_of(lax.div(block, columns) * TILE, TILE)
+        first = pl.multiple_of(lax.rem(block, columns) * width, 128)
+        return pl.ds(row, TILE), pl.ds(first, width)
+
+    mine = lax.rem(me, half)
+    def forward_all(chunk):
+        pieces_wait(far_recv_sem.at[chunk], half - 1)
+
+        def forward(step, carry):
+            owner = ranked(step)
+
+            @pl.when(owner != mirror(me))
+            def _():
+                pltpu.make_async_remote_copy(
+                    src_ref=out_ref.at[home(chunk, owner)],
+                    dst_ref=spare.at[chunk, mine],
+                    send_sem=forward_send_sem.at[chunk],
+                    recv_sem=forward_recv_sem.at[chunk],
+                    device_id=mirror(owner),
+                    device_id_type=LOGICAL,
+                ).start()
+
+            return carry
+
+        lax.fori_loop(0, half, forward, 0)
+        spare[chunk, mine] = jnp.zeros((TILE, width), jnp.bfloat16)
 
     for chunk in range(chunks):
         pieces_wait(recv_sem.at[chunk])
@@ -292,36 +328,57 @@
             return carry
 
         lax.fori_loop(0, distinct * TILE // height, blend, 0)
-        block = chunk * workers + me
-        row = pl.multiple_of(lax.div(block, columns) * TILE, TILE)
-        first = pl.multiple_of(lax.rem(block, columns) * width, 128)
-        mine = (pl.ds(row, TILE), pl.ds(first, width))
-        out_ref[mine] = mixed[chunk, lax.rem(me, distinct)]
-
-        turned = workers // 2 if chunk == chunks - 1 else 0
-
-        def back(step, carry):
-            device = ranked(lax.rem(step + turned, workers))
-
-            @pl.when(device != me)
+        out_ref[home(chunk, me)] = mixed[chunk, mine]
+
+        def back(step, absent, sem):
+            device = ranked(step)
+
+            @pl.when(device != absent)
             def _():
                 pltpu.make_async_remote_copy(
-                    src_ref=mixed.at[chunk, lax.rem(device, distinct)],
-                    dst_ref=out_ref.at[mine],
+                    src_ref=mixed.at[chunk, lax.rem(device, half)],
+                    dst_ref=out_ref.at[home(chunk, me)],
                     send_sem=back_send_sem.at[chunk],
-                    recv_sem=back_recv_sem.at[chunk],
+                    recv_sem=sem.at[chunk],
                     device_id=device,
                     device_id_type=LOGICAL,
                 ).start()
 
+        def back_far(step, carry):
+            last = chunk == chunks - 1
+            back(step, me if last else mirror(me), back_recv_sem if last else far_recv_sem)
             return carry
 
-        lax.fori_loop(0, workers, back, 0)
+        def back_near(step, carry):
+            back(step, me, back_recv_sem)
+            return carry
+
+        if chunk == chunks - 1:
+            lax.fori_loop(half, workers, back_near, 0)
+            lax.fori_loop(0, half // 2, back_far, 0)
+            for earlier in range(chunks - 1):
+                forward_all(earlier)
+            lax.fori_loop(half // 2, half, back_far, 0)
+        else:
+            lax.fori_loop(0, half, back_far, 0)
+            lax.fori_loop(half, workers, back_near, 0)
+
+    for chunk in range(chunks - 1):
+        pieces_wait(forward_recv_sem.at[chunk], half - 1)
+        total = jnp.zeros((TILE, width), jnp.float32)
+        for k in range(half):
+            piece = spare[chunk, k].astype(jnp.float32)
+            total = total - piece if k % 2 else total + piece
+        total = jnp.where(lax.rem(me, 2) == 1, total, -total)
+        out_ref[home(chunk, mirror(me))] = total.astype(jnp.bfloat16)
 
     for chunk in range(chunks):
+        last = chunk == chunks - 1
         pieces_wait(send_sem.at[chunk])
-        pieces_wait(back_send_sem.at[chunk])
-        pieces_wait(back_recv_sem.at[chunk])
+        pieces_wait(back_send_sem.at[chunk], workers - 1 if last else workers - 2)
+        if not last:
+            pieces_wait(forward_send_sem.at[chunk], half - 1)
+        pieces_wait(back_recv_sem.at[chunk], workers - 1 if last else half - 1)
 
 
 def store(mixed_ref, moment_ref, mixed_hbm, moment_hbm, sem):
@@ -377,6 +434,10 @@
             pltpu.SemaphoreType.DMA((chunks,)),
             pltpu.SemaphoreType.DMA((chunks,)),
             pltpu.SemaphoreType.DMA((chunks,)),
+            pltpu.SemaphoreType.DMA((chunks,)),
+            pltpu.VMEM((max(1, chunks - 1), distinct, TILE, width), half),
+            pltpu.SemaphoreType.DMA((chunks,)),
+            pltpu.SemaphoreType.DMA((chunks,)),
         ],
         compiler_params=pltpu.CompilerParams(
             collective_id=0, has_side_effects=True, vmem_limit_bytes=60 * 1024 * 1024

time: 52.2 us -> 51.7 us (level)
  Pallas kernels: 51.2 us -> 50.5 us
    pallas_call x1, Pallas kernels: 49.9 us -> 49.2 us  [shards(): pl.pallas_call(functools.partial(kernel, sizes), out_shape=[pltpu.VMEM((r...]
where the time goes in v3:
time: 51.7 us; the launch traced here: 51.2 us
  Pallas kernels  50.5 us (98%)
  between operations  0.64 us (1%)
    pallas_call x1, Pallas kernels, shards(): pl.pallas_call(functools.partial(kernel, sizes), out_shape=[pltpu.VMEM((r...  49.2 us
    pallas_call x1, Pallas kernels, shards(): pl.pallas_call(store, out_shape=[jax.ShapeDtypeStruct((rows, features), h...  1.33 us

profile of v3, /device:TPU:9, one launch (start us, length us, event | category | flops | bytes accessed | tf_op | source)
XLA Modules:
  0.0 51.2 jit_solution(13506719606112395761)
XLA Ops:
  0.6 49.2 %step_and_gossip.1 = (bf16[32,16384]{1,0:T(8,128)(2,1)S(1)}, bf16[32,16384]{1,0:T(8,128)(2,1)S(1)}) custom-call(bf16[256,16384]{1,0:T(8,128)(2,1)} %bitcast.9, bf16[32,256]{1,0:T(8,128)(2,1)} %bitcast.12, bf16[32,16384]{1,0:T(8,128)(2,1)} %bitcast.10, bf16[32,16384]{1,0:T(8,128)(2,1)} %bitcast.11, s32[1,32]{1,0:T(1,128)} %bitcast.13, s32[8]{0:T(128)} %shift_hbm.1), custom_call_target="tpu_custom_call" | custom-call | tf_op jit(solution)/shard_map/step_and_gossip/pallas_call | solution.py:412
  49.8 1.3 %store.1 = (bf16[32,16384]{1,0:T(8,128)(2,1)}, bf16[32,16384]{1,0:T(8,128)(2,1)}) custom-call(bf16[32,16384]{1,0:T(8,128)(2,1)S(1)} %get-tuple-element.6.mixed_ref, bf16[32,16384]{1,0:T(8,128)(2,1)S(1)} %get-tuple-element.7.moment_ref), custom_call_target="tpu_custom_call" | custom-call | tf_op jit(solution)/shard_map/store/pallas_call | solution.py:447

commit v4 on v3

--- a/solution.py
+++ b/solution.py
@@ -49,6 +49,7 @@
     load_sem,
     grad_sem,
     table_sem,
+    line_sem,
     hub_sem,
     all_sem,
     send_sem,
@@ -91,7 +92,8 @@
         turn = my_line ^ ((lines - lax.div(order, layers)) & (lines - 1))
         layer = lax.rem(order, layers)
         if columns == workers:
-            layer = layer ^ ((side ^ (1 - lax.div(group, side_groups))) * (size_x - 1))
+            far = 1 - lax.div(group, side_groups)
+            layer = layer ^ my_x ^ (far * (size_x - 1))
         return layer * lines + turn
 
     def loads(group):
@@ -117,12 +119,44 @@
     def signal(sem, device):
         pl.semaphore_signal(sem, inc=1, device_id=device, device_id_type=LOGICAL)
 
-    mates = size_x * GROUP - 1
-
-    def greet(step, carry):
-        mate = mates - step
-        signal(barrier, me ^ (lax.div(mate, GROUP) * plane + lax.rem(mate, GROUP)))
-        return carry
+    def mirror(device):
+        return device ^ ((size_x - 1) * plane)
+
+    half_x = size_x // 2
+    lead_x = side * (size_x - 1)
+    right_lead = my_x == size_x - 1
+    leader = jnp.logical_or(hub, right_lead)
+    left_inner = jnp.logical_and(my_x > 0, my_x < half_x)
+    right_inner = jnp.logical_and(my_x >= half_x, my_x < size_x - 1)
+    lead = me ^ ((my_x ^ lead_x) * plane)
+
+    def greet_side(step, carry):
+        signal(barrier, me ^ ((step + 1) * plane))
+        signal(barrier, me ^ ((step + 1) * plane) ^ 1)
+        return carry
+
+    def tell_side(step, carry):
+        signal(line_sem, me ^ ((step + 1) * plane))
+        return carry
+
+    def greet():
+        signal(barrier, mirror(me))
+        signal(barrier, mirror(me) ^ 1)
+        signal(barrier, me ^ 1)
+
+        @pl.when(jnp.logical_not(leader))
+        def _():
+            signal(barrier, lead)
+            signal(barrier, lead ^ 1)
+
+        @pl.when(hub)
+        def _():
+            lax.fori_loop(0, half_x - 1, greet_side, 0)
+            lax.fori_loop(0, lines - 1, greet_hub, 0)
+
+    others = 2 * (half_x - 1)
+    expected = 3 + jnp.where(leader, others, 0) + jnp.where(left_inner, 2, 0)
+    expected = expected + jnp.where(hub, lines - 1, 0)
 
     def greet_hub(step, carry):
         signal(barrier, me ^ ((step + 1) * GROUP))
@@ -133,7 +167,7 @@
         return carry
 
     def tell_line(step, carry):
-        signal(all_sem, me + (step + 1) * plane)
+        signal(all_sem, me ^ ((step + 1) * plane))
         return carry
 
     grad_copy = pltpu.make_async_copy(grad_hbm, grad_ref, grad_sem.at[0])
@@ -143,11 +177,7 @@
     ]
     grad_copy.start()
     load(0, 0)
-    lax.fori_loop(0, mates, greet, 0)
-
-    @pl.when(hub)
-    def _():
-        lax.fori_loop(0, lines - 1, greet_hub, 0)
+    greet()
     lax.fori_loop(1, groups, load, 0)
     for copy in table_copies:
         copy.start()
@@ -214,18 +244,60 @@
 
     grad_copy.wait()
     compute(jnp.int32(0))
-    pl.semaphore_wait(barrier, mates + jnp.where(hub, lines - 1, 0))
+    pl.semaphore_wait(barrier, expected)
+
+    @pl.when(left_inner)
+    def _():
+        signal(line_sem, lead)
 
     @pl.when(hub)
     def _():
+        pl.semaphore_wait(line_sem, half_x - 1)
+
+    @pl.when(leader)
+    def _():
+        lax.fori_loop(0, half_x - 1, tell_side, 0)
+
+    @pl.when(hub)
+    def _():
         lax.fori_loop(0, lines - 1, tell_hub, 0)
 
-    send_parts(early, jnp.int32(0))
-    for group in range(1, layers):
+    def send_all(group):
+        send_parts(early, jnp.int32(group))
+        send_parts(late, jnp.int32(group))
+
+    if columns == workers:
+        send_all(0)
+    compute(jnp.int32(1))
+
+    @pl.when(jnp.logical_not(leader))
+    def _():
+        pl.semaphore_wait(line_sem, 1)
+
+    @pl.when(right_inner)
+    def _():
+        signal(line_sem, lead)
+
+    @pl.when(right_lead)
+    def _():
+        pl.semaphore_wait(line_sem, half_x - 1)
+
+    if half_x > 2:
+
+        @pl.when(right_lead)
+        def _():
+            lax.fori_loop(0, half_x - 1, tell_side, 0)
+
+        @pl.when(right_inner)
+        def _():
+            pl.semaphore_wait(line_sem, 1)
+
+    if columns != workers:
+        send_all(0)
+    send_all(1)
+    for group in range(2, layers):
         compute(jnp.int32(group))
-        send_parts(early, jnp.int32(group))
-    for group in range(layers):
-        send_parts(late, jnp.int32(group))
+        send_all(group)
     ahead = min(layers + 4, groups - 1)
     lax.fori_loop(layers, ahead, compute_ahead, 0)
 
@@ -281,9 +353,6 @@
     def pieces_wait(sem, count=workers - 1):
         ref = recv.at[0, pl.ds(0, count)]
         pltpu.make_async_copy(ref, ref, sem).wait()
-
-    def mirror(device):
-        return device ^ ((size_x - 1) * plane)
 
     def home(chunk, owner):
         block = chunk * workers + owner
@@ -430,6 +499,7 @@
             pltpu.SemaphoreType.DMA((2,)),
             pltpu.SemaphoreType.REGULAR,
             pltpu.SemaphoreType.REGULAR,
+            pltpu.SemaphoreType.REGULAR,
             pltpu.SemaphoreType.DMA((chunks,)),
             pltpu.SemaphoreType.DMA((chunks,)),
             pltpu.SemaphoreType.DMA((chunks,)),

time: 51.7 us -> 51.1 us (0.988)
  no operation moved by 1% of the time
where the time goes in v4:
time: 51.1 us; the launch traced here: 50.8 us
  Pallas kernels  50.1 us (98%)
  between operations  0.64 us (1%)
    pallas_call x1, Pallas kernels, shards(): pl.pallas_call(functools.partial(kernel, sizes), out_shape=[pltpu.VMEM((r...  48.8 us
    pallas_call x1, Pallas kernels, shards(): pl.pallas_call(store, out_shape=[jax.ShapeDtypeStruct((rows, features), h...  1.33 us

profile of v4, /device:TPU:9, one launch (start us, length us, event | category | flops | bytes accessed | tf_op | source)
XLA Modules:
  0.0 50.8 jit_solution(7100085532082138377)
XLA Ops:
  0.6 48.8 %step_and_gossip.1 = (bf16[32,16384]{1,0:T(8,128)(2,1)S(1)}, bf16[32,16384]{1,0:T(8,128)(2,1)S(1)}) custom-call(bf16[256,16384]{1,0:T(8,128)(2,1)} %bitcast.9, bf16[32,256]{1,0:T(8,128)(2,1)} %bitcast.12, bf16[32,16384]{1,0:T(8,128)(2,1)} %bitcast.10, bf16[32,16384]{1,0:T(8,128)(2,1)} %bitcast.11, s32[1,32]{1,0:T(1,128)} %bitcast.13, s32[8]{0:T(128)} %shift_hbm.1), custom_call_target="tpu_custom_call" | custom-call | tf_op jit(solution)/shard_map/step_and_gossip/pallas_call | solution.py:481
  49.4 1.3 %store.1 = (bf16[32,16384]{1,0:T(8,128)(2,1)}, bf16[32,16384]{1,0:T(8,128)(2,1)}) custom-call(bf16[32,16384]{1,0:T(8,128)(2,1)S(1)} %get-tuple-element.6.mixed_ref, bf16[32,16384]{1,0:T(8,128)(2,1)S(1)} %get-tuple-element.7.moment_ref), custom_call_target="tpu_custom_call" | custom-call | tf_op jit(solution)/shard_map/store/pallas_call | solution.py:517

commit v5 on v4

--- a/solution.py
+++ b/solution.py
@@ -11,6 +11,7 @@
 beta_keep = 0.9
 TILE = 16
 GROUP = 2
+BANK = 4
 LOGICAL = pl.DeviceIdType.LOGICAL
 
 
@@ -47,19 +48,16 @@
     mixed,
     spread,
     load_sem,
-    grad_sem,
     table_sem,
     line_sem,
     hub_sem,
     all_sem,
-    send_sem,
+    sent_sem,
     recv_sem,
-    back_send_sem,
     back_recv_sem,
     far_recv_sem,
+    forward_recv_sem,
     spare,
-    forward_send_sem,
-    forward_recv_sem,
 ):
     size_x, size_y, size_z = sizes
     workers = size_x * size_y * size_z
@@ -96,11 +94,19 @@
             layer = layer ^ my_x ^ (far * (size_x - 1))
         return layer * lines + turn
 
-    def loads(group):
+    def bank(group):
+        return GROUP + lax.div(group + BANK - 2, BANK)
+
+    def loads(group, first=0, count=GROUP, sem=None):
         place = pair(group)
-        cut = pl.ds(pl.multiple_of(place * span, 128), span)
+        take = count * width
+        cut = pl.ds(pl.multiple_of(place * span + first * width, 128), take)
         return [
-            pltpu.make_async_copy(source.at[:, cut], kept.at[place], load_sem.at[group])
+            pltpu.make_async_copy(
+                source.at[:, cut],
+                kept.at[place, :, pl.ds(first * width, take)],
+                load_sem.at[bank(group) if sem is None else sem],
+            )
             for source, kept in (
                 (hidden_hbm, hidden),
                 (moment_hbm, moment),
@@ -112,6 +118,9 @@
         for copy in loads(group):
             copy.start()
         return carry
+
+    def single(k):
+        return loads(0, k, 1, k)
 
     barrier = pltpu.get_barrier_semaphore()
     hub = my_x == 0
@@ -170,14 +179,18 @@
         signal(all_sem, me ^ ((step + 1) * plane))
         return carry
 
-    grad_copy = pltpu.make_async_copy(grad_hbm, grad_ref, grad_sem.at[0])
+    grad_copy = pltpu.make_async_copy(grad_hbm, grad_ref, load_sem.at[0])
     table_copies = [
         pltpu.make_async_copy(held_hbm, held_ref, table_sem.at[0]),
-        pltpu.make_async_copy(shift_hbm, shift_ref, table_sem.at[1]),
+        pltpu.make_async_copy(shift_hbm, shift_ref, table_sem.at[0]),
     ]
     grad_copy.start()
-    load(0, 0)
+    for copy in single(0):
+        copy.start()
     greet()
+    for k in range(1, GROUP):
+        for copy in single(k):
+            copy.start()
     lax.fori_loop(1, groups, load, 0)
     for copy in table_copies:
         copy.start()
@@ -194,7 +207,7 @@
             pltpu.make_async_remote_copy(
                 src_ref=stage.at[part, where],
                 dst_ref=recv.at[chunk, slot],
-                send_sem=send_sem.at[chunk],
+                send_sem=sent_sem.at[0],
                 recv_sem=recv_sem.at[chunk],
                 device_id=device,
                 device_id_type=LOGICAL,
@@ -203,22 +216,39 @@
     early = [part for part in range(parts) if place_of(part, 0)[0] == 0]
     late = [part for part in range(parts) if place_of(part, 0)[0] > 0]
 
-    def compute(group):
-        place = pair(group)
-        for copy in loads(group):
-            copy.wait()
-        grad = exact_dot(grad_ref[...], hidden[place])
-        velocity = beta_keep * moment[place].astype(jnp.float32) + grad
-        cut = pl.ds(pl.multiple_of(place * span, 128), span)
+    def advance(place, first, count):
+        low, take = first * width, count * width
+        kept = (place, slice(None), slice(low, low + take))
+        velocity = beta_keep * moment[kept].astype(jnp.float32) + exact_dot(
+            grad_ref[...], hidden[kept]
+        )
+        cut = pl.ds(pl.multiple_of(place * span + low, 128), take)
         new_moment_ref[:, cut] = velocity.astype(jnp.bfloat16)
-        stepped = (weight[place].astype(jnp.float32) - learn_rate * velocity).astype(
+        stepped = (weight[kept].astype(jnp.float32) - learn_rate * velocity).astype(
             jnp.bfloat16
         )
-        for k in range(GROUP):
+        for k in range(count):
             for part in range(parts):
-                stage[part, place * GROUP + k] = stepped[
+                stage[part, place * GROUP + first + k] = stepped[
                     part * TILE : (part + 1) * TILE, k * width : (k + 1) * width
                 ]
+
+    def compute(group):
+        @pl.when((group < 2) | (lax.rem(group + BANK - 2, BANK) == 0))
+        def _():
+            for step in range(BANK):
+
+                @pl.when((bank(group + step) == bank(group)) & (group + step < groups))
+                def _():
+                    for copy in loads(group + step):
+                        copy.wait()
+
+        advance(pair(group), 0, GROUP)
+
+    def compute_single(k):
+        for copy in single(k):
+            copy.wait()
+        advance(pair(0), k, 1)
 
     def send_parts(which, group):
         for k in range(GROUP):
@@ -243,7 +273,7 @@
         return carry
 
     grad_copy.wait()
-    compute(jnp.int32(0))
+    compute_single(0)
     pl.semaphore_wait(barrier, expected)
 
     @pl.when(left_inner)
@@ -266,8 +296,12 @@
         send_parts(early, jnp.int32(group))
         send_parts(late, jnp.int32(group))
 
-    if columns == workers:
-        send_all(0)
+    for k in range(GROUP):
+        if k:
+            compute_single(k)
+        if columns == workers:
+            for part in range(parts):
+                send(part, pair(0) * GROUP + k)
     compute(jnp.int32(1))
 
     @pl.when(jnp.logical_not(leader))
@@ -372,7 +406,7 @@
                 pltpu.make_async_remote_copy(
                     src_ref=out_ref.at[home(chunk, owner)],
                     dst_ref=spare.at[chunk, mine],
-                    send_sem=forward_send_sem.at[chunk],
+                    send_sem=sent_sem.at[0],
                     recv_sem=forward_recv_sem.at[chunk],
                     device_id=mirror(owner),
                     device_id_type=LOGICAL,
@@ -407,7 +441,7 @@
                 pltpu.make_async_remote_copy(
                     src_ref=mixed.at[chunk, lax.rem(device, half)],
                     dst_ref=out_ref.at[home(chunk, me)],
-                    send_sem=back_send_sem.at[chunk],
+                    send_sem=sent_sem.at[0],
                     recv_sem=sem.at[chunk],
                     device_id=device,
                     device_id_type=LOGICAL,
@@ -423,14 +457,14 @@
             return carry
 
         if chunk == chunks - 1:
+            lax.fori_loop(0, half // 2, back_far, 0)
             lax.fori_loop(half, workers, back_near, 0)
-            lax.fori_loop(0, half // 2, back_far, 0)
             for earlier in range(chunks - 1):
                 forward_all(earlier)
             lax.fori_loop(half // 2, half, back_far, 0)
         else:
+            lax.fori_loop(half, workers, back_near, 0)
             lax.fori_loop(0, half, back_far, 0)
-            lax.fori_loop(half, workers, back_near, 0)
 
     for chunk in range(chunks - 1):
         pieces_wait(forward_recv_sem.at[chunk], half - 1)
@@ -443,10 +477,10 @@
 
     for chunk in range(chunks):
         last = chunk == chunks - 1
-        pieces_wait(send_sem.at[chunk])
-        pieces_wait(back_send_sem.at[chunk], workers - 1 if last else workers - 2)
+        for count in (workers - 1, workers - 1 if last else workers - 2):
+            pieces_wait(sent_sem.at[0], count)
         if not last:
-            pieces_wait(forward_send_sem.at[chunk], half - 1)
+            pieces_wait(sent_sem.at[0], half - 1)
         pieces_wait(back_recv_sem.at[chunk], workers - 1 if last else half - 1)
 
 
@@ -494,20 +528,17 @@
             pltpu.VMEM((chunks, workers, TILE, width), half),
             pltpu.VMEM((chunks, distinct, TILE, width), half),
             pltpu.VMEM((distinct * TILE, workers * TILE), half),
-            pltpu.SemaphoreType.DMA((groups,)),
+            pltpu.SemaphoreType.DMA((GROUP + 1 + pl.cdiv(groups - 2, BANK),)),
             pltpu.SemaphoreType.DMA((1,)),
-            pltpu.SemaphoreType.DMA((2,)),
             pltpu.SemaphoreType.REGULAR,
             pltpu.SemaphoreType.REGULAR,
             pltpu.SemaphoreType.REGULAR,
+            pltpu.SemaphoreType.DMA((1,)),
             pltpu.SemaphoreType.DMA((chunks,)),
             pltpu.SemaphoreType.DMA((chunks,)),
-            pltpu.SemaphoreType.DMA((chunks,)),
-            pltpu.SemaphoreType.DMA((chunks,)),
-            pltpu.SemaphoreType.DMA((chunks,)),
+            pltpu.SemaphoreType.DMA((max(1, chunks - 1),)),
+            pltpu.SemaphoreType.DMA((max(1, chunks - 1),)),
             pltpu.VMEM((max(1, chunks - 1), distinct, TILE, width), half),
-            pltpu.SemaphoreType.DMA((chunks,)),
-            pltpu.SemaphoreType.DMA((chunks,)),
         ],
         compiler_params=pltpu.CompilerParams(
             collective_id=0, has_side_effects=True, vmem_limit_bytes=60 * 1024 * 1024

time: 51.1 us -> 50.7 us (level)
  no operation moved by 1% of the time
where the time goes in v5:
time: 50.7 us; the launch traced here: 50.4 us
  Pallas kernels  49.8 us (98%)
  between operations  0.64 us (1%)
    pallas_call x1, Pallas kernels, shards(): pl.pallas_call(functools.partial(kernel, sizes), out_shape=[pltpu.VMEM((r...  48.5 us
    pallas_call x1, Pallas kernels, shards(): pl.pallas_call(store, out_shape=[jax.ShapeDtypeStruct((rows, features), h...  1.33 us

profile of v5, /device:TPU:9, one launch (start us, length us, event | category | flops | bytes accessed | tf_op | source)
XLA Modules:
  0.0 50.4 jit_solution(17223400672297990940)
XLA Ops:
  0.6 48.5 %step_and_gossip.1 = (bf16[32,16384]{1,0:T(8,128)(2,1)S(1)}, bf16[32,16384]{1,0:T(8,128)(2,1)S(1)}) custom-call(bf16[256,16384]{1,0:T(8,128)(2,1)} %bitcast.9, bf16[32,256]{1,0:T(8,128)(2,1)} %bitcast.12, bf16[32,16384]{1,0:T(8,128)(2,1)} %bitcast.10, bf16[32,16384]{1,0:T(8,128)(2,1)} %bitcast.11, s32[1,32]{1,0:T(1,128)} %bitcast.13, s32[8]{0:T(128)} %shift_hbm.1), custom_call_target="tpu_custom_call" | custom-call | tf_op jit(solution)/shard_map/step_and_gossip/pallas_call | solution.py:515
  49.1 1.3 %store.1 = (bf16[32,16384]{1,0:T(8,128)(2,1)}, bf16[32,16384]{1,0:T(8,128)(2,1)}) custom-call(bf16[32,16384]{1,0:T(8,128)(2,1)S(1)} %get-tuple-element.6.mixed_ref, bf16[32,16384]{1,0:T(8,128)(2,1)S(1)} %get-tuple-element.7.moment_ref), custom_call_target="tpu_custom_call" | custom-call | tf_op jit(solution)/shard_map/store/pallas_call | solution.py:548

commit v6 on v5

--- a/solution.py
+++ b/solution.py
@@ -82,7 +82,9 @@
         far = 1 - lax.div(step, half)
         turn = (side ^ far) * (size_x - 1)
         layer = lax.div(lax.rem(step, half), plane) ^ turn
-        return layer * plane + ((me & (plane - 1)) ^ (plane - 1 - lax.rem(step, plane)))
+        turn_step = lax.rem(step, plane)
+        low = ((me & (plane - 1)) ^ (plane - 1 - turn_step)) & (plane - 2)
+        return layer * plane + low + (turn_step & 1)
 
     def pair(group):
         side_groups = layers * lines

time: 50.7 us -> 50.6 us (level)
  no operation moved by 1% of the time
where the time goes in v6:
time: 50.6 us; the launch traced here: 50.5 us
  Pallas kernels  49.8 us (98%)
  between operations  0.64 us (1%)
    pallas_call x1, Pallas kernels, shards(): pl.pallas_call(functools.partial(kernel, sizes), out_shape=[pltpu.VMEM((r...  48.5 us
    pallas_call x1, Pallas kernels, shards(): pl.pallas_call(store, out_shape=[jax.ShapeDtypeStruct((rows, features), h...  1.33 us

profile of v6, /device:TPU:9, one launch (start us, length us, event | category | flops | bytes accessed | tf_op | source)
XLA Modules:
  0.0 50.5 jit_solution(10759411332054709386)
XLA Ops:
  0.6 48.5 %step_and_gossip.1 = (bf16[32,16384]{1,0:T(8,128)(2,1)S(1)}, bf16[32,16384]{1,0:T(8,128)(2,1)S(1)}) custom-call(bf16[256,16384]{1,0:T(8,128)(2,1)} %bitcast.9, bf16[32,256]{1,0:T(8,128)(2,1)} %bitcast.12, bf16[32,16384]{1,0:T(8,128)(2,1)} %bitcast.10, bf16[32,16384]{1,0:T(8,128)(2,1)} %bitcast.11, s32[1,32]{1,0:T(1,128)} %bitcast.13, s32[8]{0:T(128)} %shift_hbm.1), custom_call_target="tpu_custom_call" | custom-call | tf_op jit(solution)/shard_map/step_and_gossip/pallas_call | solution.py:517
  49.1 1.3 %store.1 = (bf16[32,16384]{1,0:T(8,128)(2,1)}, bf16[32,16384]{1,0:T(8,128)(2,1)}) custom-call(bf16[32,16384]{1,0:T(8,128)(2,1)S(1)} %get-tuple-element.6.mixed_ref, bf16[32,16384]{1,0:T(8,128)(2,1)S(1)} %get-tuple-element.7.moment_ref), custom_call_target="tpu_custom_call" | custom-call | tf_op jit(solution)/shard_map/store/pallas_call | solution.py:550

commit v7 on v6

--- a/solution.py
+++ b/solution.py
@@ -12,6 +12,7 @@
 TILE = 16
 GROUP = 2
 BANK = 4
+SLICES = 4
 LOGICAL = pl.DeviceIdType.LOGICAL
 
 
@@ -99,15 +100,12 @@
     def bank(group):
         return GROUP + lax.div(group + BANK - 2, BANK)
 
-    def loads(group, first=0, count=GROUP, sem=None):
+    def loads(group):
         place = pair(group)
-        take = count * width
-        cut = pl.ds(pl.multiple_of(place * span + first * width, 128), take)
+        cut = pl.ds(pl.multiple_of(place * span, 128), span)
         return [
             pltpu.make_async_copy(
-                source.at[:, cut],
-                kept.at[place, :, pl.ds(first * width, take)],
-                load_sem.at[bank(group) if sem is None else sem],
+                source.at[:, cut], kept.at[place], load_sem.at[bank(group)]
             )
             for source, kept in (
                 (hidden_hbm, hidden),
@@ -122,7 +120,22 @@
         return carry
 
     def single(k):
-        return loads(0, k, 1, k)
+        place = pair(0)
+        cut = pl.ds(pl.multiple_of(place * span + k * width, 128), width)
+        lanes = pl.ds(k * width, width)
+        tokens = hidden.shape[1] // SLICES
+        copies = []
+        for step in range(SLICES):
+            some = pl.ds(step * tokens, tokens)
+            source, kept = hidden_hbm.at[some, cut], hidden.at[place, some, lanes]
+            copies.append(pltpu.make_async_copy(source, kept, load_sem.at[k]))
+        for source, kept in ((moment_hbm, moment), (weight_hbm, weight)):
+            copies.append(
+                pltpu.make_async_copy(
+                    source.at[:, cut], kept.at[place, :, lanes], load_sem.at[k]
+                )
+            )
+        return copies
 
     barrier = pltpu.get_barrier_semaphore()
     hub = my_x == 0

time: 50.6 us -> 50.6 us (level)
  no operation moved by 1% of the time
where the time goes in v7:
time: 50.6 us; the launch traced here: 50.5 us
  Pallas kernels  49.8 us (98%)
  between operations  0.64 us (1%)
    pallas_call x1, Pallas kernels, shards(): pl.pallas_call(functools.partial(kernel, sizes), out_shape=[pltpu.VMEM((r...  48.5 us
    pallas_call x1, Pallas kernels, shards(): pl.pallas_call(store, out_shape=[jax.ShapeDtypeStruct((rows, features), h...  1.33 us

profile of v7, /device:TPU:9, one launch (start us, length us, event | category | flops | bytes accessed | tf_op | source)
XLA Modules:
  0.0 50.5 jit_solution(11730139791847026032)
XLA Ops:
  0.6 48.5 %step_and_gossip.1 = (bf16[32,16384]{1,0:T(8,128)(2,1)S(1)}, bf16[32,16384]{1,0:T(8,128)(2,1)S(1)}) custom-call(bf16[256,16384]{1,0:T(8,128)(2,1)} %bitcast.9, bf16[32,256]{1,0:T(8,128)(2,1)} %bitcast.12, bf16[32,16384]{1,0:T(8,128)(2,1)} %bitcast.10, bf16[32,16384]{1,0:T(8,128)(2,1)} %bitcast.11, s32[1,32]{1,0:T(1,128)} %bitcast.13, s32[8]{0:T(128)} %shift_hbm.1), custom_call_target="tpu_custom_call" | custom-call | tf_op jit(solution)/shard_map/step_and_gossip/pallas_call | solution.py:530
  49.1 1.3 %store.1 = (bf16[32,16384]{1,0:T(8,128)(2,1)}, bf16[32,16384]{1,0:T(8,128)(2,1)}) custom-call(bf16[32,16384]{1,0:T(8,128)(2,1)S(1)} %get-tuple-element.6.mixed_ref, bf16[32,16384]{1,0:T(8,128)(2,1)S(1)} %get-tuple-element.7.moment_ref), custom_call_target="tpu_custom_call" | custom-call | tf_op jit(solution)/shard_map/store/pallas_call | solution.py:563

commit v8 on v6

--- a/solution.py
+++ b/solution.py
@@ -334,7 +334,7 @@
     for group in range(2, layers):
         compute(jnp.int32(group))
         send_all(group)
-    ahead = min(layers + 4, groups - 1)
+    ahead = min(layers + 1, groups - 1)
     lax.fori_loop(layers, ahead, compute_ahead, 0)
 
     @pl.when(hub)
@@ -401,7 +401,7 @@
         pieces_wait(far_recv_sem.at[chunk], half - 1)
 
         def forward(step, carry):
-            owner = ranked(step)
+            owner = ranked(step ^ 1)
 
             @pl.when(owner != mirror(me))
             def _():

time: 50.6 us -> 50.6 us (level)
  no operation moved by 1% of the time
where the time goes in v8:
time: 50.6 us; the launch traced here: 50.5 us
  Pallas kernels  49.8 us (98%)
  between operations  0.64 us (1%)
    pallas_call x1, Pallas kernels, shards(): pl.pallas_call(functools.partial(kernel, sizes), out_shape=[pltpu.VMEM((r...  48.5 us
    pallas_call x1, Pallas kernels, shards(): pl.pallas_call(store, out_shape=[jax.ShapeDtypeStruct((rows, features), h...  1.33 us

profile of v8, /device:TPU:9, one launch (start us, length us, event | category | flops | bytes accessed | tf_op | source)
XLA Modules:
  0.0 50.5 jit_solution(9929628279124527064)
XLA Ops:
  0.6 48.5 %step_and_gossip.1 = (bf16[32,16384]{1,0:T(8,128)(2,1)S(1)}, bf16[32,16384]{1,0:T(8,128)(2,1)S(1)}) custom-call(bf16[256,16384]{1,0:T(8,128)(2,1)} %bitcast.9, bf16[32,256]{1,0:T(8,128)(2,1)} %bitcast.12, bf16[32,16384]{1,0:T(8,128)(2,1)} %bitcast.10, bf16[32,16384]{1,0:T(8,128)(2,1)} %bitcast.11, s32[1,32]{1,0:T(1,128)} %bitcast.13, s32[8]{0:T(128)} %shift_hbm.1), custom_call_target="tpu_custom_call" | custom-call | tf_op jit(solution)/shard_map/step_and_gossip/pallas_call | solution.py:517
  49.1 1.3 %store.1 = (bf16[32,16384]{1,0:T(8,128)(2,1)}, bf16[32,16384]{1,0:T(8,128)(2,1)}) custom-call(bf16[32,16384]{1,0:T(8,128)(2,1)S(1)} %get-tuple-element.6.mixed_ref, bf16[32,16384]{1,0:T(8,128)(2,1)S(1)} %get-tuple-element.7.moment_ref), custom_call_target="tpu_custom_call" | custom-call | tf_op jit(solution)/shard_map/store/pallas_call | solution.py:550
